TPU v7x, 32 devices: a whole 2x2x4 slice. The times are simulated.
32 devices in a mesh: dp: 2 (over x), tp: 4 (over z), ep: 4 (over y, core).
Axes of the slice: x: 2, y: 2, z: 4, core: 2. Of those that a mesh axis runs over, the one named last changes fastest.
Arguments:
- x: bfloat16 [2048, 2048], P(('dp', 'tp', 'ep')), parts along dimension 0
- route_idx: int32 [2048, 8], P(('dp', 'tp', 'ep')), parts along dimension 0
- gates: float32 [2048, 8], P(('dp', 'tp', 'ep')), parts along dimension 0
- w1: bfloat16 [64, 2048, 1024], P('ep', None, 'tp')
- w3: bfloat16 [64, 2048, 1024], P('ep', None, 'tp')
- w2: bfloat16 [64, 1024, 2048], P('ep', 'tp')
Outputs:
- output: bfloat16 [2048, 2048], P(('dp', 'tp', 'ep')), parts along dimension 0
There are 2 independent parts. A program takes and returns all parts, laid end to end along the dimension named above; an argument that names none is the same for every part.
All inputs are finite; a program needn't handle non-finite values.
Results may differ from a plain program's by a relative error of at most 0.00782163.
Values are sent between devices in bfloat16 or wider.
A program may use at most 1 GiB of HBM per device.

v0:
```python
import jax
import jax.numpy as jnp
from jax import lax
from jax.sharding import PartitionSpec as P


def solution(mesh):
    tp = mesh.shape['tp']
    ep = mesh.shape['ep']
    tok_spec = P(('dp', 'tp', 'ep'), None)

    def local(x, route_idx, gates, w1, w3, w2):
        t_loc, d = x.shape
        top = route_idx.shape[1]
        e_loc = w1.shape[0]
        n_exp = e_loc * ep
        cap = t_loc // 2
        hit = jnp.any(route_idx[:, :, None] == jnp.arange(n_exp, dtype=jnp.int32)[None, None, :], axis=1)
        pos = jnp.cumsum(hit.astype(jnp.int32), axis=0) - 1
        dest = route_idx * cap + jnp.take_along_axis(pos, route_idx, axis=1)
        src = jnp.full((n_exp * cap,), t_loc, jnp.int32).at[dest.reshape(-1)].set(
            jnp.repeat(jnp.arange(t_loc, dtype=jnp.int32), top))
        xp = jnp.concatenate([x, jnp.zeros((1, d), x.dtype)], axis=0)
        send = xp[src].reshape(ep, e_loc * cap, d)
        recv = lax.all_to_all(send, 'ep', 0, 0, tiled=True)
        full = lax.all_gather(recv, 'tp', axis=0, tiled=False)
        rows = full.reshape(tp, ep, e_loc, cap, d).transpose(2, 0, 1, 3, 4).reshape(e_loc, tp * ep * cap, d)
        a = jnp.einsum('erd,edf->erf', rows, w1, preferred_element_type=jnp.float32)
        b = jnp.einsum('erd,edf->erf', rows, w3, preferred_element_type=jnp.float32)
        h = (jax.nn.silu(a) * b).astype(jnp.bfloat16)
        o = jnp.einsum('erf,efd->erd', h, w2, preferred_element_type=jnp.float32)
        o = o.reshape(e_loc, tp, ep, cap, d).transpose(1, 2, 0, 3, 4)
        o = lax.psum_scatter(o, 'tp', scatter_dimension=0, tiled=True)
        o = o.reshape(ep, e_loc * cap, d).astype(jnp.bfloat16)
        back = lax.all_to_all(o, 'ep', 0, 0, tiled=True).reshape(n_exp * cap, d)
        got = back[dest].astype(jnp.float32)
        y = jnp.sum(got * gates[:, :, None], axis=1)
        return y.astype(jnp.bfloat16)

    return jax.shard_map(local, mesh=mesh,
                         in_specs=(tok_spec, tok_spec, tok_spec, P('ep', None, 'tp'), P('ep', None, 'tp'), P('ep', 'tp', None)),
                         out_specs=tok_spec, check_vma=False)
```

profile of v0, /device:TPU:0, one launch (start us, length us, event | category | flops | bytes accessed | tf_op | source)
XLA Modules:
  0.0 2048.7 jit_solution(7129569000991853510)
XLA Ops:
  6.5 0.8 copy.42
  7.3 0.7 bitcast_or_fusion
  8.0 0.2 fusion.5
  8.2 0.1 reduce_window_sum.11
  8.4 0.1 reshape.86
  8.5 3.8 gather_fusion.2
  12.4 0.6 compare_select_fusion.2
  13.1 0.1 reshape.63
  13.3 2.4 scatter_custom_fusion
  15.8 11.0 gather_fusion
  26.9 101.0 %all_to_all.10 = bf16[4,512,2048]{2,1,0:T(8,128)(2,1)} all-to-all(bf16[4,512,2048]{2,1,0:T(8,128)(2,1)} %bitcast.33), channel_id=1, replica_groups=mesh['dp'=2,'tp'=4,'ep'=4] {'ep'}, dimensions={0} | all-to-all | bytes 16777216 | tf_op jit(solution)/shard_map/all_to_all | solution.py:25
  127.8 0.2 reduce-scatter.2.cloned.1.call-start
  128.1 563.4 %all-gather.3.cloned.1.call-done = bf16[16,512,2048]{2,1,0:T(8,128)(2,1)} async-done(((bf16[4,512,2048]{2,1,0:T(8,128)(2,1)}), bf16[16,512,2048]{2,1,0:T(8,128)(2,1)}) %all-gather.3.cloned.1.call-update) | async-done | bytes 33554448 | tf_op jit(solution)/shard_map/all_gather | solution.py:26
  691.5 22.9 %copy.46 = bf16[16,4,4,32,2048]{4,3,2,1,0:T(8,128)(2,1)} copy(bf16[16,4,4,32,2048]{4,3,0,2,1:T(8,128)(2,1)} %bitcast.34) | data formatting | bytes 67108864 | tf_op jit(solution)/shard_map/transpose | solution.py:27
  714.4 22.9 %fusion.10 = f32[16,512,256]{2,1,0:T(8,128)} fusion(bf16[16,512,2048]{2,1,0:T(8,128)(2,1)} %bitcast.35, bf16[16,2048,256]{2,1,0:T(8,128)(2,1)} %param.9), kind=kOutput, calls=%fused_computation.25 | convolution fusion | flops 8589934592 | bytes 58720256 | tf_op jit(solution)/shard_map/erd,edf->erf/dot_general | solution.py:28
  737.4 23.7 %multiply_convert_fusion.4 = bf16[16,512,256]{2,1,0:T(8,128)(2,1)} fusion(f32[16,512,256]{2,1,0:T(8,128)} %fusion.10, bf16[16,512,2048]{2,1,0:T(8,128)(2,1)} %bitcast.36, bf16[16,2048,256]{2,1,0:T(8,128)(2,1)} %param.10), kind=kOutput, calls=%fused_computation.5.clone.clone.1 | convolution fusion | flops 8602517504 | bytes 62914560 | tf_op jit(solution)/shard_map/erd,edf->erf/dot_general | solution.py:29
  761.1 30.0 %fusion = f32[16,512,2048]{2,1,0:T(8,128)} fusion(bf16[16,256,2048]{2,1,0:T(8,128)(2,1)} %param.11, bf16[16,512,256]{2,1,0:T(8,128)(2,1)} %multiply_convert_fusion.4), kind=kOutput, calls=%fused_computation.6 | convolution fusion | flops 8589934592 | bytes 88080384 | tf_op jit(solution)/shard_map/erf,efd->erd/dot_general | solution.py:31
  791.0 44.7 %copy.51 = f32[16,4,4,32,2048]{4,3,0,2,1:T(8,128)} copy(f32[16,4,4,32,2048]{4,3,2,1,0:T(8,128)} %bitcast.6) | data formatting | bytes 134217728 | tf_op jit(solution)/shard_map/reshape | solution.py:32
  835.8 1086.9 %reduce-scatter.2.cloned.1.call-done = f32[1,4,16,32,2048]{4,3,2,1,0:T(8,128)} async-done(((f32[4,4,16,32,2048]{4,3,2,1,0:T(8,128)}), f32[1,4,16,32,2048]{4,3,2,1,0:T(8,128)}) %reduce-scatter.2.cloned.1.call-update) | async-done | bytes 16777232 | tf_op jit(solution)/shard_map/reduce_scatter | solution.py:33
  1922.7 9.1 convert_element_type.20
  1931.8 6.0 all-to-all-start.1
  1938.1 92.3 %all-to-all-done.1 = bf16[4,512,2048]{2,1,0:T(8,128)(2,1)} async-done(((bf16[4,512,2048]{2,1,0:T(8,128)(2,1)}), bf16[4,512,2048]{2,1,0:T(8,128)(2,1)}, u32[]{:S(2)}, u32[]{:S(2)}) %all-to-all-start.1) | async-done | bytes 8388640 | tf_op jit(solution)/shard_map/all_to_all | solution.py:35
  2030.4 8.9 gather_fusion.1
  2039.3 2.5 fusion.3
  (26 shorter events, 0.8 us)
Async XLA Ops:
  6.5 685.0 %all-gather.3.cloned.1.call-start = ((), (), s32[]{:S(2)}) async-start(), calls=%async_computation.4 | async-start | bytes 41943040 | tf_op jit(solution)/shard_map/all_gather | solution.py:26
  8.5 3.9 copy-start.1
  8.5 7.3 copy-start
  127.8 1794.9 %reduce-scatter.2.cloned.1.call-start = ((), (), s32[]{:S(2)}) async-start(), calls=%async_computation.3 | async-start | bytes 83886080 | tf_op jit(solution)/shard_map/reduce_scatter | solution.py:33
  1931.8 6.0 copy-start.2
  1931.8 6.2 copy-start.3
  1931.8 98.6 %all-to-all-start.1 = ((bf16[4,512,2048]{2,1,0:T(8,128)(2,1)}), bf16[4,512,2048]{2,1,0:T(8,128)(2,1)}, u32[]{:S(2)}, u32[]{:S(2)}) async-start(bf16[4,512,2048]{2,1,0:T(8,128)(2,1)} %bitcast.32), calls=%async_computation.2 | async-start | bytes 16777216 | tf_op jit(solution)/shard_map/all_to_all | solution.py:35
Sparse Core Ops, SparseCore 0:
  128.0 563.4 all-gather.2
  835.9 1086.7 reduce-scatter.1
where the time goes:
time: 2050 us
  waiting for transfers between devices  1740 us (85%)
  blocking collectives  101 us (5%)
  local copies, waits for them, and re-layouts  95.4 us (5%)
  matrix products  76.6 us (4%)
    reduce_scatter x1, waiting for transfers between devices, local(): o = lax.psum_scatter(o, 'tp', scatter_dimension=0, tiled=True)  1090 us
    all_gather x1, waiting for transfers between devices, local(): full = lax.all_gather(recv, 'tp', axis=0, tiled=False)  563 us
    all_to_all x1, blocking collectives, local(): recv = lax.all_to_all(send, 'ep', 0, 0, tiled=True)  101 us
    all_to_all x1, waiting for transfers between devices, local(): back = lax.all_to_all(o, 'ep', 0, 0, tiled=True).reshape(n_exp * cap, d)  92.3 us
    reshape x1, local copies, waits for them, and re-layouts, local(): o = o.reshape(e_loc, tp, ep, cap, d).transpose(1, 2, 0, 3, 4)  44.7 us
  transfers between devices with their start and end apart: 3, of which 3 were waited for; matrix products, arithmetic and copies ran while one was open for 0% of the time, Pallas kernels for 0%

commit v1 on v0

v1 whole, which is shorter than its diff:
```python
import functools

import jax
import jax.numpy as jnp
from jax import lax
from jax.experimental import pallas as pl
from jax.experimental.pallas import tpu as pltpu
from jax.sharding import PartitionSpec as P

TM = 128
BR = 16
LAG = 2
NS = LAG + 1
NO = NS + 1
TC = 256
SIZES = (640, 768, 896, 1024, 1152, 1280, 1408, 1536, 1792, 2304)
MESH = pl.DeviceIdType.MESH


def expert_kernel(meta, dest, x, w1, w3, w2, out, obuf, cnt, sem):
    e = pl.program_id(0)
    n_tok = x.shape[0]

    def drain(slot):
        def one(_, c):
            pltpu.make_async_copy(obuf.at[slot, pl.ds(0, 8)], out.at[0, pl.ds(0, 8)], sem.at[slot]).wait()
            return c
        lax.fori_loop(0, cnt[slot], one, 0)

    @pl.when(e == 0)
    def _():
        cnt[0] = 0
        cnt[1] = 0
        cnt[2] = 0

    blocks, blocks0, off0, off1 = meta[e, 0], meta[e, 1], meta[e, 2], meta[e, 3]

    def tile(i, c):
        rows = lax.broadcasted_iota(jnp.int32, (TM, n_tok), 0) + i * TM
        pick = jnp.where(dest[0] == rows, 1.0, 0.0).astype(jnp.bfloat16)
        xs = jnp.dot(pick, x[...], preferred_element_type=jnp.float32).astype(jnp.bfloat16)
        a = jnp.dot(xs, w1[0], preferred_element_type=jnp.float32)
        b = jnp.dot(xs, w3[0], preferred_element_type=jnp.float32)
        h = (jax.nn.silu(a) * b).astype(jnp.bfloat16)
        slot = cnt[2]
        drain(slot)
        obuf[slot] = jnp.dot(h, w2[0], preferred_element_type=jnp.float32)
        first = i * (TM // 8)
        n = jnp.minimum(TM // 8, blocks - first)

        def put(k, c):
            g = first + k
            late = g >= blocks0
            half = jnp.where(late, 1, 0)
            to = jnp.where(late, off1 + g - blocks0, off0 + g)
            pltpu.make_async_copy(
                obuf.at[slot, pl.ds(pl.multiple_of(k * 8, 8), 8)],
                out.at[half, pl.ds(pl.multiple_of(to * 8, 8), 8)], sem.at[slot]).start()
            return c

        lax.fori_loop(0, n, put, 0)
        cnt[slot] = n
        cnt[2] = 1 - slot
        return c

    lax.fori_loop(0, (blocks + TM // 8 - 1) // (TM // 8), tile, 0)

    @pl.when(e == pl.num_programs(0) - 1)
    def _():
        drain(0)
        drain(1)


def chain_kernel(n, blocks, src, out, own, rbuf, sbuf, obuf, own_sem, send_sem, recv_sem, out_sem, credit):
    z = lax.axis_index('tp')
    barrier = pltpu.get_barrier_semaphore()

    @pl.when(z > 0)
    def _():
        pl.semaphore_signal(barrier, inc=1, device_id={'tp': z - 1}, device_id_type=MESH)

    @pl.when(z < n - 1)
    def _():
        pl.semaphore_signal(barrier, inc=1, device_id={'tp': z + 1}, device_id_type=MESH)

    pl.semaphore_wait(barrier, jnp.where(z > 0, 1, 0) + jnp.where(z < n - 1, 1, 0))

    def load(d, k):
        s = lax.rem(k, NO)
        return pltpu.make_async_copy(src.at[1 - d, pl.ds(pl.multiple_of(k * BR, BR), BR)], own.at[d, s], own_sem.at[d, s])

    def send(d, k, buf, s_buf):
        s = lax.rem(k, NS)
        to = z + 1 if d == 0 else z - 1
        return pltpu.make_async_remote_copy(
            src_ref=buf.at[d, s_buf], dst_ref=rbuf.at[d, s], send_sem=send_sem.at[d, s], recv_sem=recv_sem.at[d, s],
            device_id={'tp': to}, device_id_type=MESH)

    def put(k):
        s = lax.rem(k, 2)
        return pltpu.make_async_copy(obuf.at[s], out.at[pl.ds(pl.multiple_of(k * BR, BR), BR)], out_sem.at[s])

    def step(i, c):
        work = []
        for d in (0, 1):
            p = z if d == 0 else n - 1 - z
            k = i - LAG * p
            work.append((d, p, k, jnp.logical_and(k >= 0, k < blocks)))

        for d, p, k, live in work:
            @pl.when(live)
            def _(d=d, p=p, k=k):
                @pl.when(jnp.logical_and(p < n - 1, k >= NS))
                def _():
                    send(d, k - NS, sbuf, lax.rem(k, NS)).wait_send()

                @pl.when(k == 0)
                def _():
                    load(d, k).start()

                @pl.when(k + 1 < blocks)
                def _():
                    load(d, k + 1).start()

                load(d, k).wait()

        for d, p, k, live in work:
            @pl.when(jnp.logical_and(live, p == 0))
            def _(d=d, k=k):
                @pl.when(k >= NS)
                def _():
                    pl.semaphore_wait(credit.at[d], 1)
                send(d, k, own, lax.rem(k, NO)).start()

        for d, p, k, live in work:
            @pl.when(jnp.logical_and(live, p > 0))
            def _(d=d, p=p, k=k):
                s = lax.rem(k, NS)
                send(d, k, sbuf, s).wait_recv()

                @pl.when(p < n - 1)
                def _():
                    sbuf[d, s] = rbuf[d, s] + own[d, lax.rem(k, NO)]

                @pl.when(p == n - 1)
                def _():
                    t = lax.rem(k, 2)

                    @pl.when(k >= 2)
                    def _():
                        put(k - 2).wait()
                    obuf[t] = (rbuf[d, s] + own[d, lax.rem(k, NO)]).astype(jnp.bfloat16)
                    put(k).start()

                @pl.when(k + NS < blocks)
                def _():
                    back = z - 1 if d == 0 else z + 1
                    pl.semaphore_signal(credit.at[d], inc=1, device_id={'tp': back}, device_id_type=MESH)

        for d, p, k, live in work:
            @pl.when(jnp.logical_and(live, jnp.logical_and(p > 0, p < n - 1)))
            def _(d=d, k=k):
                @pl.when(k >= NS)
                def _():
                    pl.semaphore_wait(credit.at[d], 1)
                send(d, k, sbuf, lax.rem(k, NS)).start()
        return c

    lax.fori_loop(0, blocks + LAG * (n - 1), step, 0)

    for d in (0, 1):
        p = z if d == 0 else n - 1 - z

        @pl.when(p < n - 1)
        def _(d=d):
            for k in range(blocks - NS, blocks):
                send(d, k, sbuf, k % NS).wait_send()

        @pl.when(p == n - 1)
        def _():
            put(blocks - 2).wait()
            put(blocks - 1).wait()


def combine_kernel(count, rows, gates, src, out, obuf, sem):
    top = rows.shape[1]
    total = count[0]
    tiles = (total + TC - 1) // TC

    def load(j, s):
        return pltpu.make_async_copy(src.at[pl.ds(pl.multiple_of(j * TC, TC), TC)], obuf.at[s], sem.at[s])

    out[...] = jnp.zeros_like(out)

    @pl.when(tiles > 0)
    def _():
        load(0, 0).start()

    def tile(j, c):
        s = lax.rem(j, 2)

        @pl.when(j + 1 < tiles)
        def _():
            load(j + 1, 1 - s).start()

        col = lax.broadcasted_iota(jnp.int32, (rows.shape[0], TC), 1) + j * TC
        g = jnp.zeros((rows.shape[0], TC), jnp.float32)
        for k in range(top):
            g = g + jnp.where(rows[:, k:k + 1] == col, gates[:, k:k + 1], 0.0)
        g1 = g.astype(jnp.bfloat16)
        rest = g - g1.astype(jnp.float32)
        g2 = rest.astype(jnp.bfloat16)
        g3 = (rest - g2.astype(jnp.float32)).astype(jnp.bfloat16)
        load(j, s).wait()
        row = lax.broadcasted_iota(jnp.int32, (TC, obuf.shape[2]), 0) + j * TC
        o = jnp.where(row < total, obuf[s].astype(jnp.float32), 0.0).astype(jnp.bfloat16)
        out[...] += jnp.dot(jnp.concatenate([g1, g2, g3], axis=1), jnp.concatenate([o, o, o], axis=0),
                            preferred_element_type=jnp.float32)
        return c

    lax.fori_loop(0, tiles, tile, 0)


def solution(mesh):
    tp = mesh.shape['tp']
    ep = mesh.shape['ep']
    tok_spec = P(('dp', 'tp', 'ep'), None)

    def local(x, route_idx, gates, w1, w3, w2):
        t_loc, d = x.shape
        top = route_idx.shape[1]
        e_loc, _, f = w1.shape
        n_tok = t_loc * tp * ep
        n_half = n_tok // 2
        z = lax.axis_index('tp')
        j = lax.axis_index('ep')
        last = (z == tp - 1)
        end = jnp.logical_or(z == 0, last)
        side = jnp.where(z >= tp // 2, 1, 0)

        info = lax.all_gather(jnp.concatenate([route_idx.astype(jnp.float32), gates], axis=1), ('tp', 'ep'), axis=0, tiled=True)
        xa = lax.all_gather(x, ('tp', 'ep'), axis=0, tiled=True)

        loc = info[:, :top].astype(jnp.int32) - j * e_loc
        ga = info[:, top:]
        ids = jnp.arange(e_loc, dtype=jnp.int32)
        hit = jnp.any(loc.T[None] == ids[:, None, None], axis=1)
        before = jnp.arange(n_half)[:, None] < jnp.arange(n_half)[None, :]
        hit2 = hit.reshape(e_loc * 2, n_half)
        pos = jnp.dot(hit2.astype(jnp.bfloat16), before.astype(jnp.bfloat16),
                      preferred_element_type=jnp.float32).astype(jnp.int32).reshape(e_loc, 2, n_half)
        n = jnp.sum(hit2.astype(jnp.int32), axis=1).reshape(e_loc, 2)
        nb = (n + 7) // 8
        off = jnp.sum(jnp.where(ids[:, None, None] > ids[None, :, None], nb[None], 0), axis=1)
        total = jnp.sum(nb, axis=0) * 8
        meta = jnp.stack([nb[:, 0] + nb[:, 1], nb[:, 0], off[:, 0], off[:, 1]], axis=1)
        base = jnp.stack([jnp.zeros_like(nb[:, 0]), nb[:, 0] * 8], axis=1)
        dest = jnp.where(hit, (base[:, :, None] + pos).reshape(e_loc, n_tok), -1)

        full = -(-(n_half * top + 7 * e_loc) // TC) * TC
        part = pl.pallas_call(
            expert_kernel,
            grid_spec=pltpu.PrefetchScalarGridSpec(
                num_scalar_prefetch=1,
                grid=(e_loc,),
                in_specs=[
                    pl.BlockSpec((1, 1, n_tok), lambda e, m: (e, 0, 0)),
                    pl.BlockSpec((n_tok, d), lambda e, m: (0, 0)),
                    pl.BlockSpec((1, d, f), lambda e, m: (e, 0, 0)),
                    pl.BlockSpec((1, d, f), lambda e, m: (e, 0, 0)),
                    pl.BlockSpec((1, f, d), lambda e, m: (e, 0, 0)),
                ],
                out_specs=pl.BlockSpec(memory_space=pl.ANY),
                scratch_shapes=[
                    pltpu.VMEM((2, TM, d), jnp.float32),
                    pltpu.SMEM((3,), jnp.int32),
                    pltpu.SemaphoreType.DMA((2,)),
                ]),
            out_shape=jax.ShapeDtypeStruct((2, full, d), jnp.float32),
            compiler_params=pltpu.CompilerParams(dimension_semantics=('arbitrary',), vmem_limit_bytes=60000 * 1024),
            name='experts',
        )(meta, dest.reshape(e_loc, 1, n_tok), xa, w1, w3, w2)

        def chain(size, ident):
            return pl.pallas_call(
                functools.partial(chain_kernel, tp, size // BR),
                in_specs=[pl.BlockSpec(memory_space=pl.ANY)],
                out_specs=pl.BlockSpec(memory_space=pl.ANY),
                out_shape=jax.ShapeDtypeStruct((full, d), jnp.bfloat16),
                scratch_shapes=[
                    pltpu.VMEM((2, NO, BR, d), jnp.float32),
                    pltpu.VMEM((2, NS, BR, d), jnp.float32),
                    pltpu.VMEM((2, NS, BR, d), jnp.float32),
                    pltpu.VMEM((2, BR, d), jnp.bfloat16),
                    pltpu.SemaphoreType.DMA((2, NO)),
                    pltpu.SemaphoreType.DMA((2, NS)),
                    pltpu.SemaphoreType.DMA((2, NS)),
                    pltpu.SemaphoreType.DMA((2,)),
                    pltpu.SemaphoreType.REGULAR((2,)),
                ],
                compiler_params=pltpu.CompilerParams(collective_id=ident, has_side_effects=True, vmem_limit_bytes=60000 * 1024),
                name=f'chain{size}',
            )

        sizes = tuple(s for s in SIZES if s < full) + (full,)
        need = jnp.max(total)
        which = jnp.sum((need > jnp.array(sizes[:-1], jnp.int32)).astype(jnp.int32))
        o = lax.switch(which, [chain(s, i + 1) for i, s in enumerate(sizes)], part)

        row = (off[:, :, None] * 8 + pos)[:, side]
        mine = loc.reshape(2, n_half, top)[side]
        same = mine[:, :, None] == ids[None, None, :]
        rows = jnp.sum(jnp.where(same, row.T[:, None, :], 0), axis=2)
        rows = jnp.where(jnp.any(same, axis=2), rows, -1)
        order = lambda v: v.reshape(tp // 2, ep, t_loc, top).transpose(1, 0, 2, 3).reshape(n_half, top)
        count = jnp.where(end, total[side], 0).reshape(1)
        py = pl.pallas_call(
            combine_kernel,
            in_specs=[
                pl.BlockSpec(memory_space=pltpu.SMEM),
                pl.BlockSpec(memory_space=pltpu.VMEM),
                pl.BlockSpec(memory_space=pltpu.VMEM),
                pl.BlockSpec(memory_space=pl.ANY),
            ],
            out_specs=pl.BlockSpec(memory_space=pltpu.VMEM),
            out_shape=jax.ShapeDtypeStruct((n_half, d), jnp.float32),
            scratch_shapes=[pltpu.VMEM((2, TC, d), jnp.bfloat16), pltpu.SemaphoreType.DMA((2,))],
            compiler_params=pltpu.CompilerParams(vmem_limit_bytes=60000 * 1024),
            name='combine',
        )(count, order(rows), order(ga.reshape(2, n_half, top)[side]), o)

        y = lax.psum_scatter(py.reshape(ep, n_half // ep, d), 'ep', scatter_dimension=0, tiled=False)
        y = y.astype(jnp.bfloat16).reshape(2, t_loc, d)
        own = jnp.where(last, y[1], y[0])
        got = lax.ppermute(jnp.where(last, y[0], y[1]), 'tp', [(0, 1), (tp - 1, tp - 2)])
        return jnp.where(end, own, got)

    return jax.shard_map(local, mesh=mesh,
                         in_specs=(tok_spec, tok_spec, tok_spec, P('ep', None, 'tp'), P('ep', None, 'tp'), P('ep', 'tp', None)),
                         out_specs=tok_spec, check_vma=False)
```

time: 2050 us -> 419 us (0.20)
  waiting for transfers between devices: 1740 us -> 67.9 us
  Pallas kernels: 0 us -> 299 us
  local copies, waits for them, and re-layouts: 95.4 us -> 3.36 us
  blocking collectives: 101 us -> 23.7 us
  matrix products: 76.6 us -> 0.2 us
    reduce_scatter x1, waiting for transfers between devices: 1090 us -> 41.3 us  [local(): lax.psum_scatter(py.reshape(ep, n_half // ep, d), 'ep', scatter_dimension...]
    all_gather x1, waiting for transfers between devices: 563 us -> 20.6 us  [local(): xa = lax.all_gather(x, ('tp', 'ep'), axis=0, tiled=True)]
    pallas_call x0 -> x3, Pallas kernels: none -> 299 us  [the longest x1 232 us: local(): o = lax.switch(which, [chain(s, i + 1) for i, s in enumerate(sizes)], part)]
    all_to_all x1 -> x0, blocking collectives: 101 us -> none  [local(): recv = lax.all_to_all(send, 'ep', 0, 0, tiled=True)]
    all_to_all x1 -> x0, waiting for transfers between devices: 92.3 us -> none  [local(): back = lax.all_to_all(o, 'ep', 0, 0, tiled=True).reshape(n_exp * cap, d)]
    dot_general x3 -> x1, matrix products: 76.6 us -> 0.2 us  [local(): jnp.dot(hit2.astype(jnp.bfloat16), before.astype(jnp.bfloat16), preferred...]
    reshape x3, local copies, waits for them, and re-layouts: 44.9 us -> 0.13 us  [the longest x2 0.11 us: local(): pos = jnp.dot(hit2.astype(jnp.bfloat16), before.astype(jnp.bfloat16), pre...]
    gather x7 -> x0, local copies, waits for them, and re-layouts: 24 us -> none  [the longest x1 11 us: local(): send = xp[src].reshape(ep, e_loc * cap, d)]
  transfers between devices with their start and end apart: 3 -> 3, of which waited for: 3 -> 3; matrix products, arithmetic and copies ran while one was open for 0% -> 2% of each run, Pallas kernels for 0% -> 0%
where the time goes in v1:
time: 419 us; the launch traced here: 420 us
  Pallas kernels  299 us (71%)
  waiting for transfers between devices  67.9 us (16%)
  blocking collectives  23.7 us (6%)
  between operations  14.9 us (4%)
  other arithmetic  8.25 us (2%)
    pallas_call x1, Pallas kernels, local(): o = lax.switch(which, [chain(s, i + 1) for i, s in enumerate(sizes)], part)  232 us
    pallas_call x1, Pallas kernels, local(): pl.pallas_call(expert_kernel, grid_spec=pltpu.PrefetchScalarGridSpec(num_...  47.5 us
    reduce_scatter x1, waiting for transfers between devices, local(): lax.psum_scatter(py.reshape(ep, n_half // ep, d), 'ep', scatter_dimension...  41.3 us
    all_gather x1, blocking collectives, local(): lax.all_gather(jnp.concatenate([route_idx.astype(jnp.float32), gates], ax...  23.7 us
    all_gather x1, waiting for transfers between devices, local(): xa = lax.all_gather(x, ('tp', 'ep'), axis=0, tiled=True)  20.6 us
    pallas_call x1, Pallas kernels, local(): pl.pallas_call(combine_kernel, in_specs=[pl.BlockSpec(memory_space=pltpu....  19.1 us
  transfers between devices with their start and end apart: 3, of which 3 were waited for; matrix products, arithmetic and copies ran while one was open for 2% of the time, Pallas kernels for 0%

profile of v1, /device:TPU:0, one launch (start us, length us, event | category | flops | bytes accessed | tf_op | source)
XLA Modules:
  0.0 420.4 jit_solution(2252316144226052892)
XLA Ops:
  6.5 0.7 all-gather.3.cloned.1.call-update
  7.3 0.7 convert_element_type.21
  8.0 0.7 maximum_bitcast_fusion
  8.7 23.7 %all-gather = f32[16,64,16]{1,2,0:T(8,128)S(1)} all-gather(f32[1,64,16]{1,2,0:T(8,128)S(1)} %maximum_bitcast_fusion), channel_id=1, replica_groups=mesh['dp'=2,'tp'=4,'ep'=4] {'tp','ep'}, dimensions={0}, use_global_device_ids=true | all-gather | bytes 69632 | tf_op jit(solution)/shard_map/all_gather | solution.py:241
  32.5 0.2 fusion
  32.7 0.2 convolution_convert_fusion
  33.0 0.1 convert_reduce_fusion
  34.4 0.8 copy.37
  35.2 0.6 fusion.7
  35.9 0.6 dynamic_slice.12
  36.6 0.9 copy.38
  37.4 2.0 fusion.6
  40.8 0.7 pad_add_fusion.meta
  41.4 0.7 copy_select_fusion.dest
  42.2 20.6 %all-gather.3.cloned.1.call-done.x = bf16[1024,2048]{1,0:T(8,128)(2,1)} async-done(((bf16[64,2048]{1,0:T(8,128)(2,1)}), bf16[1024,2048]{1,0:T(8,128)(2,1)}) %all-gather.3.cloned.1.call-update) | async-done | bytes 4194320 | tf_op jit(solution)/shard_map/all_gather | solution.py:242
  62.8 47.5 %experts.1 = f32[2,4352,2048]{2,1,0:T(8,128)} custom-call(s32[16,4]{1,0:T(8,128)} %pad_add_fusion.meta, s32[16,1,1024]{2,1,0:T(1,128)} %copy_select_fusion.dest, bf16[1024,2048]{1,0:T(8,128)(2,1)} %all-gather.3.cloned.1.call-done.x, bf16[16,2048,256]{2,1,0:T(8,128)(2,1)} %w1.1, bf16[16,2048,256]{2,1,0:T(8,128)(2,1)} %w3.1, bf16[16,256,2048]{2,1,0:T(8,128)(2,1)} %w2.1), custom_call_target="tpu_custom_call" | custom-call | tf_op jit(solution)/shard_map/experts/pallas_call | solution.py:261
  110.3 232.0 %conditional.1 = (bf16[4352,2048]{1,0:T(8,128)(2,1)}) conditional(s32[]{:T(128)} %clamp.3, f32[2,4352,2048]{2,1,0:T(8,128)} %experts.1, f32[2,4352,2048]{2,1,0:T(8,128)} %experts.1, f32[2,4352,2048]{2,1,0:T(8,128)} %experts.1, f32[2,4352,2048]{2,1,0:T(8,128)} %experts.1, f32[2,4352,2048]{2,1,0:T(8,128)} %experts.1, ...), branch_computations={%region_8.9_spmd, %region_9.10_spmd, %region_10.11_spmd, %region_1... | conditional | bytes 8 | solution.py:308
  110.4 231.9 %chain1280.1 = bf16[4352,2048]{1,0:T(8,128)(2,1)} custom-call(f32[2,4352,2048]{2,1,0:T(8,128)} %src.5), custom_call_target="tpu_custom_call" | custom-call | tf_op jit(solution)/shard_map/cond/branch_5_fun/chain1280/pallas_call | solution.py:308
  342.3 19.1 %combine.1 = f32[512,2048]{1,0:T(8,128)} custom-call(s32[1]{0:T(128)} %bitcast.3.count, s32[512,8]{1,0:T(8,128)} %bitcast.32, f32[512,8]{1,0:T(8,128)} %bitcast.33, bf16[4352,2048]{1,0:T(8,128)(2,1)} %get-tuple-element.35.src), custom_call_target="tpu_custom_call" | custom-call | tf_op jit(solution)/shard_map/combine/pallas_call | solution.py:317
  361.5 41.3 %reduce-scatter.2.cloned.1.call-done = f32[1,128,2048]{2,1,0:T(8,128)} async-done(((f32[4,128,2048]{2,1,0:T(8,128)}), f32[1,128,2048]{2,1,0:T(8,128)}) %reduce-scatter.2.cloned.1.call-update) | async-done | bytes 1048592 | tf_op jit(solution)/shard_map/reduce_scatter | solution.py:332
  402.8 1.3 convert_element_type.26
  404.1 3.4 collective-permute-start
  407.5 5.3 %collective-permute-done = bf16[64,2048]{1,0:T(8,128)(2,1)S(1)} collective-permute-done((bf16[64,2048]{1,0:T(8,128)(2,1)S(1)}, bf16[64,2048]{1,0:T(8,128)(2,1)S(1)}, u32[]{:S(2)}, u32[]{:S(2)}) %collective-permute-start) | collective-permute-done | bytes 262176 | tf_op jit(solution)/shard_map/ppermute | solution.py:335
  412.8 0.8 bitcast_select_fusion
  (34 shorter events, 1.6 us)
Async XLA Ops:
  6.5 56.3 %all-gather.3.cloned.1.call-start = ((), (), s32[]{:S(2)}) async-start(), calls=%async_computation.1 | async-start | bytes 4456448 | tf_op jit(solution)/shard_map/all_gather | solution.py:242
  7.3 395.5 %reduce-scatter.2.cloned.1.call-start = ((), (), s32[]{:S(2)}) async-start(), calls=%async_computation.2 | async-start | bytes 5242880 | tf_op jit(solution)/shard_map/reduce_scatter | solution.py:332
  404.1 8.7 %collective-permute-start = (bf16[64,2048]{1,0:T(8,128)(2,1)S(1)}, bf16[64,2048]{1,0:T(8,128)(2,1)S(1)}, u32[]{:S(2)}, u32[]{:S(2)}) collective-permute-start(bf16[64,2048]{1,0:T(8,128)(2,1)S(1)} %select_bitcast_fusion), channel_id=1, source_target_pairs={{0,4},{12,8},{1,5},{13,9},{2,6},{14,10},{3,7},{15,11},{16,20},{28,... | collective-permute-start | bytes 786440 | tf_op jit(solution)/shard_map/ppermute | solution.py:335
Sparse Core Ops, SparseCore 0:
  9.5 53.2 all-gather.2
  361.6 41.1 reduce-scatter.1
